TPU v7x, 32 devices: a whole 2x2x4 slice. The times are simulated.
32 devices in a mesh: doc: 2 (over x), seq: 4 (over y, core), head: 4 (over z).
Axes of the slice: x: 2, y: 2, z: 4, core: 2. Of those that a mesh axis runs over, the one named last changes fastest.
Arguments:
- length: int32 [2], P('doc'), parts along dimension 0, may hold values from 896 to 1024
- residual: bfloat16 [2048, 4096], P(('doc', 'seq'), 'head'), parts along dimension 0, may hold values from -6 to 6
- ssm_input: bfloat16 [2048, 4096], P(('doc', 'seq'), 'head'), parts along dimension 0, may hold values from -6 to 6
- state_in: bfloat16 [2048, 128], P(('doc', 'seq')), parts along dimension 0, may hold values from -6 to 6
- state_out: bfloat16 [2048, 128], P(('doc', 'seq')), parts along dimension 0, may hold values from -0.5 to 0.5
- step_raw: float32 [128, 1024], P(('doc', 'head'), 'seq'), parts along dimension 0, may hold values from -5 to 2
- decay_rate: float32 [64], P('head'), may hold values from 0 to 1, as said below
- ssm_gain: float32 [4096], P('head'), may hold values from 0.1 to 1.9
- out_weight: bfloat16 [4096, 4096], P('head'), may hold values from -0.09375 to 0.09375
- norm_gain: float32 [4096], replicated, may hold values from 0.1 to 1.9
- query_weight: bfloat16 [4096, 4096], P(None, 'head'), may hold values from -2 to 2
- key_weight: bfloat16 [4096, 1024], P(None, 'head'), may hold values from -3 to 3
- value_weight: bfloat16 [4096, 1024], P(None, 'head'), may hold values from -0.09375 to 0.09375
Outputs:
- layer_out: bfloat16 [2048, 4096], P(('doc', 'seq'), 'head'), parts along dimension 0
- head_out: bfloat16 [2048, 4096], P(('doc', 'seq'), 'head'), parts along dimension 0
There are 2 independent parts, one for each index of `doc`. A program takes and returns all parts, laid end to end along the dimension named above; an argument that names none is the same for every part. Nothing has to cross between parts.
Inputs may be any that keep to these rules, and one draw needn't show every extreme that they name: The document fills positions 0 to length - 1 of the 1024; later positions are padding. `decay_rate`: positive.
All inputs are finite; a program needn't handle non-finite values.
Results may differ from a plain program's by a relative error of at most 0.028.
The roundings to bfloat16 on the way count: a program that leaves them out, or rounds other values in their place, can miss the bound.
Values may be sent and summed in bfloat16 or wider, within the bound.
A program may use at most 64 MiB of HBM per device.

v0:
```python
import jax
import jax.numpy as jnp
from jax import lax
from jax.sharding import PartitionSpec as P

HEAD_DIM = 128
EPSILON = 1e-05
NEG_BIG = -1e30
HIGHEST = lax.Precision.HIGHEST


def prefix_2(value, axis, join, neutral):
    count, mine = (lax.axis_size(axis), lax.axis_index(axis))
    pieces = jax.tree.map(lambda part: lax.all_gather(part, axis), value)
    so_far = jax.tree.map(
        lambda part, zero: jnp.full_like(part, 0) + jnp.asarray(zero, part.dtype), value, neutral
    )

    def turn(position, so_far):
        longer = join(so_far, jax.tree.map(lambda part: part[position], pieces))
        return jax.tree.map(lambda new, old: jnp.where(position < mine, new, old), longer, so_far)

    return lax.fori_loop(0, count - 1, turn, so_far)


def chain_link(earlier, later):
    return (earlier[0] * later[0], later[0][:, None, None] * earlier[1] + later[1])


def body(
    length,
    residual,
    ssm_input,
    state_in,
    state_out,
    step_raw,
    decay_rate,
    ssm_gain,
    out_weight,
    norm_gain,
    query_weight,
    key_weight,
    value_weight,
):
    rows = residual.shape[0]
    local_heads = decay_rate.shape[0]
    head_width = ssm_input.shape[1] // local_heads
    seq_index = lax.axis_index("seq")
    limit = length[0]
    positions = seq_index * rows + jnp.arange(rows, dtype=jnp.int32)
    live_rows = positions < limit
    live = live_rows.astype(jnp.float32)
    delta = live[None, :] * jax.nn.softplus(step_raw)
    cumlog = jnp.cumsum(-decay_rate[:, None] * delta, axis=1)
    inputs = ssm_input.astype(jnp.float32).reshape(rows, local_heads, head_width)
    inner = jnp.dot(state_out, state_in.T, preferred_element_type=jnp.float32)
    causal = jnp.arange(rows)[:, None] >= jnp.arange(rows)[None, :]
    spread = cumlog[:, :, None] - cumlog[:, None, :]
    mixing = (
        jnp.where(causal[None], jnp.exp(jnp.where(causal[None], spread, 0.0)), 0.0)
        * inner[None]
        * delta[:, None, :]
    )
    within = jnp.einsum("hts,shp->thp", mixing, inputs, precision=HIGHEST)
    tail = jnp.exp(cumlog[:, -1:] - cumlog) * delta
    local_state = jnp.einsum(
        "hs,shp,sn->hpn", tail, inputs, state_in.astype(jnp.float32), precision=HIGHEST
    )
    block_decay = jnp.exp(cumlog[:, -1])
    prefix = prefix_2(
        (block_decay, local_state),
        "seq",
        chain_link,
        (jnp.ones_like(block_decay), jnp.zeros_like(local_state)),
    )
    incoming = prefix[1]
    carried = jnp.einsum("hpn,tn->thp", incoming, state_out.astype(jnp.float32), precision=HIGHEST)
    ssm_out = (within + jnp.exp(cumlog).T[:, :, None] * carried) * live[:, None, None]
    mean_square = jnp.mean(ssm_out * ssm_out, axis=2, keepdims=True)
    normed = (
        ssm_out * lax.rsqrt(mean_square + EPSILON) * ssm_gain.reshape(local_heads, head_width)
    ).astype(jnp.bfloat16)
    normed = normed.reshape(rows, local_heads * head_width)
    partial_value = jnp.dot(normed, out_weight, preferred_element_type=jnp.float32)
    model_width = norm_gain.shape[0]
    own_width = residual.shape[1]
    projected = lax.psum_scatter(partial_value, "head", scatter_dimension=1, tiled=True)
    layer_out = (residual.astype(jnp.float32) + projected).astype(jnp.bfloat16)
    widened = layer_out.astype(jnp.float32)
    squares = lax.psum(jnp.sum(widened * widened, axis=1), "head")
    piece_gain = lax.dynamic_slice_in_dim(norm_gain, lax.axis_index("head") * own_width, own_width)
    scaled = (widened * lax.rsqrt(squares / model_width + EPSILON)[:, None] * piece_gain).astype(
        jnp.bfloat16
    )
    attn_in = lax.all_gather(scaled, "head", axis=1, tiled=True)
    queries = jnp.dot(attn_in, query_weight, preferred_element_type=jnp.float32).astype(
        jnp.bfloat16
    )
    keys = jnp.dot(attn_in, key_weight, preferred_element_type=jnp.float32).astype(jnp.bfloat16)
    values = jnp.dot(attn_in, value_weight, preferred_element_type=jnp.float32).astype(jnp.bfloat16)
    query_local = query_weight.shape[1] // HEAD_DIM
    kv_local = key_weight.shape[1] // HEAD_DIM
    group_size = query_local // kv_local
    grouped = queries.reshape(rows, kv_local, group_size, HEAD_DIM)
    best = jnp.full((rows, query_local), NEG_BIG, jnp.float32)
    key_piece = lax.all_gather(keys, "seq", axis=0, tiled=True)
    value_piece = lax.all_gather(values, "seq", axis=0, tiled=True)
    count = key_piece.shape[0]
    key_pos = jnp.arange(count, dtype=jnp.int32)
    allowed = (key_pos[None, :] <= positions[:, None]) & (key_pos[None, :] < limit)
    scores = jnp.einsum(
        "tkgd,rkd->tkgr",
        grouped,
        key_piece.reshape(count, kv_local, HEAD_DIM),
        preferred_element_type=jnp.float32,
    ) * HEAD_DIM ** (-0.5)
    scores = scores.reshape(rows, query_local, count)
    allowed_wide = allowed[:, None, :]
    masked = jnp.where(allowed_wide, scores, NEG_BIG)
    new_best = jnp.maximum(best, jnp.max(masked, axis=2))
    weights = jnp.where(allowed_wide, jnp.exp(masked - new_best[:, :, None]), 0.0)
    total = jnp.sum(weights, axis=2)
    update = jnp.einsum(
        "tkgr,rkd->tkgd",
        weights.astype(jnp.bfloat16).reshape(rows, kv_local, group_size, count),
        value_piece.reshape(count, kv_local, HEAD_DIM),
        preferred_element_type=jnp.float32,
    )
    accum = update.reshape(rows, query_local, HEAD_DIM)
    folded = (new_best, total, accum)
    total = folded[1]
    accum = folded[2]
    safe_total = jnp.where(live_rows[:, None], total, 1.0)
    head_out = (
        (accum / safe_total[:, :, None] * live[:, None, None])
        .astype(jnp.bfloat16)
        .reshape(rows, query_local * HEAD_DIM)
    )
    return (layer_out, head_out)


def solution(mesh):
    placed = (
        P("doc"),
        P(("doc", "seq"), "head"),
        P(("doc", "seq"), "head"),
        P(("doc", "seq"), None),
        P(("doc", "seq"), None),
        P(("doc", "head"), "seq"),
        P("head"),
        P("head"),
        P("head", None),
        P(),
        P(None, "head"),
        P(None, "head"),
        P(None, "head"),
    )
    return jax.shard_map(
        body,
        mesh=mesh,
        in_specs=placed,
        out_specs=(P(("doc", "seq"), "head"), P(("doc", "seq"), "head")),
        check_vma=False,
    )
```

profile of v0, /device:TPU:0, one launch (start us, length us, event | category | flops | bytes accessed | tf_op | source)
XLA Modules:
  0.0 233.8 jit_solution(13353778681474807331)
XLA Ops:
  8.0 0.7 neg.8
  8.7 0.8 multiply_bitcast_fusion.1
  9.5 0.6 reduce-window.6
  10.0 0.2 slice_reduce_fusion
  10.2 0.1 copy_bitcast_fusion
  10.3 0.2 slice_reduce_fusion.1
  10.5 1.2 copy.34
  11.8 0.1 exponential_bitcast_fusion
  11.9 2.3 fusion.31
  14.2 0.0 reduce-scatter.2.cloned.1.call-start
  14.2 0.8 mul.159
  15.0 1.2 dynamic-slice
  16.9 0.2 dynamic-update-slice
  17.1 8.4 %all-reduce = f32[64]{0:T(128)S(1)} all-reduce(f32[64]{0:T(128)S(1)} %dynamic-update-slice), channel_id=2, replica_groups=mesh['doc'=2,'seq'=4,'head'=4] {'seq'}, use_global_device_ids=true, to_apply=%add | all-reduce | flops 64 | bytes 512
  25.5 0.1 reshape.196
  25.6 1.1 fusion.48
  26.7 4.4 %fusion.20 = f32[256,16,64]{0,2,1:T(8,128)} fusion(bf16[256,16,64]{0,2,1:T(8,128)(2,1)S(1)} %bitcast.100, f32[16,256]{1,0:T(8,128)S(1)} %get-tuple-element.130, f32[256,256]{1,0:T(8,128)S(1)} %fusion.48, f32[16,256]{1,0:T(8,128)S(1)} %copy_bitcast_fusion, pred[256,256]{1,0:T(8,128)(4,1)S(1)} %iota_compare_fusion.1), kind=kOutput, calls=%fused_computation.24 | convolution fusion | flops 810549248 | bytes 1933312 | tf_op jit(solution)/shard_map/hts,shp->thp/dot_general | solution.py:64
  31.1 8.5 %all-gather.7.cloned.1.call-done = f32[64,64,128]{2,1,0:T(8,128)} async-done(((f32[16,64,128]{2,1,0:T(8,128)}), f32[64,64,128]{2,1,0:T(8,128)}) %all-gather.7.cloned.1.call-update) | async-done | bytes 2097168 | tf_op jit(solution)/shard_map/all_gather | solution.py:14
  39.6 3.6 %while.14 = (s32[]{:T(128)}, f32[16,64,128]{2,1,0:T(8,128)S(1)}, s32[]{:T(128)}, f32[4,16]{1,0:T(4,128)S(1)}, f32[4,16,64,128]{3,2,1,0:T(8,128)}, /*index=5*/s32[]{:T(128)}, s32[]{:T(128)}) while((s32[]{:T(128)}, f32[16,64,128]{2,1,0:T(8,128)S(1)}, s32[]{:T(128)}, f32[4,16]{1,0:T(4,128)S(1)}, f32[4,16,64,128]{3,2,1,0:T(8,128)}, ...), condition=%wide.region_3.4_spmd.clone, body=%wide.region_2.3_spmd.clone.sunk | while | flops 524292 | bytes 1573169 | solution.py:23
  39.6 1.2 fusion.64
  40.8 1.2 fusion.64
  42.1 1.2 fusion.64
  43.2 1.9 multiply_reduce_fusion
  45.1 0.2 multiply_convert_fusion
  45.4 7.7 %fusion.49 = f32[256,4096]{1,0:T(8,128)} fusion(bf16[256,1024]{0,1:T(8,128)(2,1)S(1)} %bitcast.98, bf16[1024,4096]{1,0:T(8,128)(2,1)} %param.23), kind=kOutput, calls=%fused_computation.78 | convolution fusion | flops 2147483648 | bytes 13107200 | tf_op jit(solution)/shard_map/dot_general | solution.py:84
  53.1 0.0 all-gather.5.cloned.1.call-start
  53.1 0.7 dynamic_slice.17
  53.9 76.2 %reduce-scatter.2.cloned.1.call-done = f32[256,1024]{1,0:T(8,128)} async-done(((f32[256,4096]{1,0:T(8,128)}), f32[256,1024]{1,0:T(8,128)}) %reduce-scatter.2.cloned.1.call-update) | async-done | bytes 1048592 | tf_op jit(solution)/shard_map/reduce_scatter | solution.py:87
  130.0 1.5 fusion.26
  131.5 11.0 %psum.7 = f32[256]{0:T(256)S(1)} all-reduce(f32[256]{0:T(256)S(1)} %get-tuple-element.127), channel_id=1, replica_groups=mesh['doc'=2,'seq'=4,'head'=4] {'head'}, use_global_device_ids=true, to_apply=%region_7.8 | all-reduce | flops 256 | bytes 2048 | tf_op jit(solution)/shard_map/psum | solution.py:90
  142.5 1.0 fusion.28
  143.5 0.2 fusion.34
  143.8 43.9 %all-gather.5.cloned.1.call-done = bf16[256,4096]{1,0:T(8,128)(2,1)} async-done(((bf16[256,1024]{1,0:T(8,128)(2,1)}), bf16[256,4096]{1,0:T(8,128)(2,1)}) %all-gather.5.cloned.1.call-update) | async-done | bytes 2097168 | tf_op jit(solution)/shard_map/all_gather | solution.py:95
  187.7 6.3 %convolution_convert_fusion = bf16[256,1024]{1,0:T(8,128)(2,1)S(1)} fusion(bf16[256,4096]{1,0:T(8,128)(2,1)} %all-gather.5.cloned.1.call-done, bf16[4096,1024]{1,0:T(8,128)(2,1)} %param.25), kind=kOutput, calls=%fused_computation.30 | convolution fusion | flops 2147745792 | bytes 11010048 | tf_op jit(solution)/shard_map/dot_general | solution.py:96
  194.0 1.2 reshape.194
  195.2 2.3 convolution_convert_fusion.2
  197.5 7.2 %all_gather.23 = bf16[1024,256]{1,0:T(8,128)(2,1)S(1)} all-gather(bf16[256,256]{1,0:T(8,128)(2,1)S(1)} %convolution_convert_fusion.2), channel_id=1, replica_groups=mesh['doc'=2,'seq'=4,'head'=4] {'seq'}, dimensions={0}, use_global_device_ids=true | all-gather | bytes 655360 | tf_op jit(solution)/shard_map/all_gather | solution.py:107
  204.6 0.2 copy.44
  204.9 2.9 %convolution_convert_fusion.1 = bf16[256,256]{1,0:T(8,128)(2,1)S(1)} fusion(bf16[256,4096]{1,0:T(8,128)(2,1)} %all-gather.5.cloned.1.call-done, bf16[4096,256]{1,0:T(8,128)(2,1)} %param.26), kind=kOutput, calls=%fused_computation.31 | convolution fusion | flops 536936448 | bytes 4325376 | tf_op jit(solution)/shard_map/dot_general | solution.py:99
  207.8 7.5 %all_gather.24 = bf16[1024,256]{1,0:T(8,128)(2,1)S(1)} all-gather(bf16[256,256]{1,0:T(8,128)(2,1)S(1)} %convolution_convert_fusion.1), channel_id=1, replica_groups=mesh['doc'=2,'seq'=4,'head'=4] {'seq'}, dimensions={0}, use_global_device_ids=true | all-gather | bytes 655360 | tf_op jit(solution)/shard_map/all_gather | solution.py:106
  215.3 0.9 reshape.193
  216.2 2.7 %fusion.1 = (f32[256,2,4]{0,2,1:T(4,128)S(1)}, f32[2,1024,256,4]{2,1,3,0:T(8,128)S(1)}) fusion(pred[256,1024]{0,1:T(8,128)(4,1)S(1)} %fusion.34, bf16[256,2,4,128]{3,2,1,0:T(4,128)(2,1)} %reshape.194, bf16[1024,2,128,1]{2,1,0,3:T(2,128)(2,1)} %bitcast.103), kind=kOutput, calls=%fused_computation.5 | convolution fusion | flops 543160320 | bytes 9707520 | tf_op jit(solution)/shard_map/tkgd,rkd->tkgr/dot_general | solution.py:111
  218.9 2.0 fusion.2
  220.9 3.2 %fusion.11 = f32[2,128,256,4]{2,1,3,0:T(8,128)} fusion(bf16[1024,2,128,1]{0,2,3,1:T(8,128)(2,1)S(1)} %bitcast.102, f32[2,1024,256,4]{2,1,3,0:T(8,128)S(1)} %get-tuple-element.138, f32[256,2,4]{0,2,1:T(4,128)S(1)} %broadcast_maximum_fusion, pred[256,1024]{0,1:T(8,128)(4,1)S(1)} %fusion.34), kind=kOutput, calls=%fused_computation.15 | convolution fusion | flops 547356672 | bytes 10231808 | tf_op jit(solution)/shard_map/tkgr,rkd->tkgd/dot_general | solution.py:123
  224.1 1.6 copy.40
  225.7 0.1 copy.39
  225.9 0.3 div.27
  226.2 1.0 fusion.30
  (29 shorter events, 0.3 us)
Async XLA Ops:
  7.2 188.0 %copy-start = (bf16[4096,256]{1,0:T(8,128)(2,1)S(1)}, bf16[4096,256]{1,0:T(8,128)(2,1)}, u32[]{:S(2)}) copy-start(bf16[4096,256]{1,0:T(8,128)(2,1)} %param.27) | copy-start | bytes 6291460
  7.2 32.4 %all-gather.7.cloned.1.call-start = ((), (), s32[]{:S(2)}) async-start(), calls=%async_computation.3 | async-start | bytes 2621440 | tf_op jit(solution)/shard_map/all_gather | solution.py:14
  14.2 115.8 %reduce-scatter.2.cloned.1.call-start = ((), (), s32[]{:S(2)}) async-start(), calls=%async_computation.1 | async-start | bytes 5242880 | tf_op jit(solution)/shard_map/reduce_scatter | solution.py:87
  31.1 12.2 %copy-start.3 = (bf16[256,128]{1,0:T(8,128)(2,1)S(1)}, bf16[256,128]{1,0:T(8,128)(2,1)}, u32[]{:S(2)}) copy-start(bf16[256,128]{1,0:T(8,128)(2,1)} %param.19) | copy-start | bytes 196612
  53.0 77.0 %copy-start.2 = (bf16[256,1024]{1,0:T(8,128)(2,1)S(1)}, bf16[256,1024]{1,0:T(8,128)(2,1)}, u32[]{:S(2)}) copy-start(bf16[256,1024]{1,0:T(8,128)(2,1)} %param.16) | copy-start | bytes 1572868
  53.1 134.6 %all-gather.5.cloned.1.call-start = ((), (), s32[]{:S(2)}) async-start(), calls=%async_computation.2 | async-start | bytes 2621440 | tf_op jit(solution)/shard_map/all_gather | solution.py:95
  131.5 62.5 %copy-start.1 = (bf16[256,1024]{1,0:T(8,128)(2,1)}, bf16[256,1024]{1,0:T(8,128)(2,1)S(1)}, u32[]{:S(2)}) copy-start(bf16[256,1024]{1,0:T(8,128)(2,1)S(1)} %get-tuple-element.128) | copy-start | bytes 1572868
Sparse Core Ops, SparseCore 0:
  14.3 25.2 all-gather.6
  53.2 76.7 reduce-scatter.1
  143.6 43.9 all-gather.4
where the time goes:
time: 235 us; the launch traced here: 234 us
  waiting for transfers between devices  129 us (55%)
  matrix products  34.8 us (15%)
  blocking collectives  34 us (14%)
  between operations  15.4 us (7%)
  other arithmetic  11.7 us (5%)
  local copies, waits for them, and re-layouts  9.02 us (4%)
    reduce_scatter x1, waiting for transfers between devices, body(): lax.psum_scatter(partial_value, 'head', scatter_dimension=1, tiled=True)  76.2 us
    all_gather x1, waiting for transfers between devices, body(): attn_in = lax.all_gather(scaled, 'head', axis=1, tiled=True)  43.9 us
    psum x1, blocking collectives, body(): squares = lax.psum(jnp.sum(widened * widened, axis=1), 'head')  11 us
    all_gather x1, waiting for transfers between devices, prefix_2(): pieces = jax.tree.map(lambda part: lax.all_gather(part, axis), value)  8.54 us
    unnamed x1, blocking collectives  8.37 us
    dot_general x1, matrix products, body(): jnp.dot(normed, out_weight, preferred_element_type=jnp.float32)  7.69 us
    all_gather x1, blocking collectives, body(): key_piece = lax.all_gather(keys, 'seq', axis=0, tiled=True)  7.46 us
    all_gather x1, blocking collectives, body(): value_piece = lax.all_gather(values, 'seq', axis=0, tiled=True)  7.15 us
  transfers between devices with their start and end apart: 3, of which 3 were waited for; matrix products, arithmetic and copies ran while one was open for 4% of the time, Pallas kernels for 0%

commit v1 on v0

--- a/solution.py
+++ b/solution.py
@@ -92,7 +92,14 @@
     scaled = (widened * lax.rsqrt(squares / model_width + EPSILON)[:, None] * piece_gain).astype(
         jnp.bfloat16
     )
-    attn_in = lax.all_gather(scaled, "head", axis=1, tiled=True)
+    n_dev = lax.axis_size("head")
+    right = [(i, (i + 1) % n_dev) for i in range(n_dev)]
+    parts = [scaled]
+    for stride in range(1, n_dev):
+        parts = [lax.ppermute(parts[0], "head", right), *parts]
+    whole = jnp.concatenate(parts, axis=1)
+    shift = (lax.axis_index("head") + 1) * parts[-1].shape[1]
+    attn_in = jnp.roll(whole, shift, axis=1)
     queries = jnp.dot(attn_in, query_weight, preferred_element_type=jnp.float32).astype(
         jnp.bfloat16
     )

time: 235 us -> 226 us (0.962)
  matrix products: 34.8 us -> 27 us
  waiting for transfers between devices: 129 us -> 123 us
  local copies, waits for them, and re-layouts: 9.02 us -> 14.5 us
    all_gather x1 -> x0, waiting for transfers between devices: 43.9 us -> none  [body(): attn_in = lax.all_gather(scaled, 'head', axis=1, tiled=True)]
    ppermute x0 -> x3, waiting for transfers between devices: none -> 38.3 us  [body(): parts = [lax.ppermute(parts[0], 'head', right), *parts]]
    unnamed x12 -> x24, local copies, waits for them, and re-layouts: 2.76 us -> 8.2 us
    dot_general x1, matrix products: 6.34 us -> 2.32 us  [body(): jnp.dot(attn_in, query_weight, preferred_element_type=jnp.float32)]
  transfers between devices with their start and end apart: 3 -> 5, of which waited for: 3 -> 5; matrix products, arithmetic and copies ran while one was open for 4% -> 4% of each run, Pallas kernels for 0% -> 0%
where the time goes in v1:
time: 226 us; the launch traced here: 225 us
  waiting for transfers between devices  123 us (54%)
  blocking collectives  33.6 us (15%)
  matrix products  27 us (12%)
  between operations  15.8 us (7%)
  local copies, waits for them, and re-layouts  14.5 us (6%)
  other arithmetic  11.3 us (5%)
    reduce_scatter x1, waiting for transfers between devices, body(): lax.psum_scatter(partial_value, 'head', scatter_dimension=1, tiled=True)  76.2 us
    ppermute x3, waiting for transfers between devices, body(): parts = [lax.ppermute(parts[0], 'head', right), *parts]  38.3 us
    psum x1, blocking collectives, body(): squares = lax.psum(jnp.sum(widened * widened, axis=1), 'head')  11 us
    all_gather x1, waiting for transfers between devices, prefix_2(): pieces = jax.tree.map(lambda part: lax.all_gather(part, axis), value)  8.54 us
    unnamed x1, blocking collectives  8.37 us
    unnamed x24, local copies, waits for them, and re-layouts  8.2 us
    dot_general x1, matrix products, body(): jnp.dot(normed, out_weight, preferred_element_type=jnp.float32)  7.69 us
    all_gather x1, blocking collectives, body(): key_piece = lax.all_gather(keys, 'seq', axis=0, tiled=True)  7.28 us
  transfers between devices with their start and end apart: 5, of which 5 were waited for; matrix products, arithmetic and copies ran while one was open for 4% of the time, Pallas kernels for 0%

profile of v1, /device:TPU:0, one launch (start us, length us, event | category | flops | bytes accessed | tf_op | source)
XLA Modules:
  0.0 225.4 jit_solution(4119998479374276725)
XLA Ops:
  8.0 0.7 neg.8
  8.7 0.8 multiply_bitcast_fusion.1
  9.5 0.6 reduce-window.6
  10.3 0.2 slice_reduce_fusion.1
  10.5 1.2 copy.34
  11.9 2.3 %fusion.46 = f32[16,64,128]{2,1,0:T(8,128)} fusion(bf16[256,16,64]{0,2,1:T(8,128)(2,1)S(1)} %bitcast.96, f32[256,16]{0,1:T(8,128)S(1)} %get-tuple-element.134, bf16[256,128]{1,0:T(8,128)(2,1)} %param.18), kind=kOutput, calls=%fused_computation.49 | convolution fusion | flops 403177472 | bytes 1130496 | tf_op jit(solution)/shard_map/hs,shp,sn->hpn/dot_general | solution.py:66
  14.2 0.8 mul.162
  15.0 1.2 dynamic-slice
  16.9 0.2 dynamic-update-slice
  17.1 8.4 %all-reduce = f32[64]{0:T(128)S(1)} all-reduce(f32[64]{0:T(128)S(1)} %dynamic-update-slice), channel_id=2, replica_groups=mesh['doc'=2,'seq'=4,'head'=4] {'seq'}, use_global_device_ids=true, to_apply=%add | all-reduce | flops 64 | bytes 512
  25.6 1.1 fusion.66
  26.7 4.4 %fusion.26 = f32[256,16,64]{0,2,1:T(8,128)} fusion(bf16[256,16,64]{0,2,1:T(8,128)(2,1)S(1)} %bitcast.97, f32[16,256]{1,0:T(8,128)S(1)} %get-tuple-element.130, f32[256,256]{1,0:T(8,128)S(1)} %fusion.66, f32[16,256]{1,0:T(8,128)S(1)} %copy_bitcast_fusion, pred[256,256]{1,0:T(8,128)(4,1)S(1)} %iota_compare_fusion.1), kind=kOutput, calls=%fused_computation.30 | convolution fusion | flops 810549248 | bytes 1933312 | tf_op jit(solution)/shard_map/hts,shp->thp/dot_general | solution.py:64
  31.1 8.5 %all-gather.4.cloned.1.call-done = f32[64,64,128]{2,1,0:T(8,128)} async-done(((f32[16,64,128]{2,1,0:T(8,128)}), f32[64,64,128]{2,1,0:T(8,128)}) %all-gather.4.cloned.1.call-update) | async-done | bytes 2097168 | tf_op jit(solution)/shard_map/all_gather | solution.py:14
  39.6 3.6 %while.14 = (s32[]{:T(128)}, f32[16,64,128]{2,1,0:T(8,128)S(1)}, s32[]{:T(128)}, f32[4,16]{1,0:T(4,128)S(1)}, f32[4,16,64,128]{3,2,1,0:T(8,128)}, /*index=5*/s32[]{:T(128)}, s32[]{:T(128)}) while((s32[]{:T(128)}, f32[16,64,128]{2,1,0:T(8,128)S(1)}, s32[]{:T(128)}, f32[4,16]{1,0:T(4,128)S(1)}, f32[4,16,64,128]{3,2,1,0:T(8,128)}, ...), condition=%wide.region_3.4_spmd.clone, body=%wide.region_2.3_spmd.clone.sunk | while | flops 524292 | bytes 1573169 | solution.py:23
  39.6 1.2 fusion.79
  40.8 1.2 fusion.79
  42.1 1.2 fusion.79
  43.2 1.9 multiply_reduce_fusion
  45.1 0.2 multiply_convert_fusion
  45.3 7.7 %fusion.67 = f32[256,4096]{1,0:T(8,128)} fusion(bf16[256,1024]{0,1:T(8,128)(2,1)S(1)} %bitcast.95, bf16[1024,4096]{1,0:T(8,128)(2,1)} %param.23), kind=kOutput, calls=%fused_computation.95 | convolution fusion | flops 2147483648 | bytes 13107200 | tf_op jit(solution)/shard_map/dot_general | solution.py:84
  53.1 0.7 dynamic_slice.21
  53.8 76.2 %reduce-scatter.2.cloned.1.call-done = f32[256,1024]{1,0:T(8,128)} async-done(((f32[256,4096]{1,0:T(8,128)}), f32[256,1024]{1,0:T(8,128)}) %reduce-scatter.2.cloned.1.call-update) | async-done | bytes 1048592 | tf_op jit(solution)/shard_map/reduce_scatter | solution.py:87
  130.0 1.5 fusion.41
  131.5 11.0 %psum.7 = f32[256]{0:T(256)S(1)} all-reduce(f32[256]{0:T(256)S(1)} %get-tuple-element.127), channel_id=1, replica_groups=mesh['doc'=2,'seq'=4,'head'=4] {'head'}, use_global_device_ids=true, to_apply=%region_7.8 | all-reduce | flops 256 | bytes 2048 | tf_op jit(solution)/shard_map/psum | solution.py:90
  142.5 0.2 fusion.43
  142.8 13.6 %collective-permute-done = bf16[256,1024]{1,0:T(8,128)(2,1)S(1)} collective-permute-done((bf16[256,1024]{1,0:T(8,128)(2,1)S(1)}, bf16[256,1024]{1,0:T(8,128)(2,1)S(1)}, u32[]{:S(2)}, u32[]{:S(2)}) %collective-permute-start) | collective-permute-done | bytes 524320 | tf_op jit(solution)/shard_map/ppermute | solution.py:99
  156.3 12.8 %collective-permute-done.1 = bf16[256,1024]{1,0:T(8,128)(2,1)} collective-permute-done((bf16[256,1024]{1,0:T(8,128)(2,1)S(1)}, bf16[256,1024]{1,0:T(8,128)(2,1)}, u32[]{:S(2)}, u32[]{:S(2)}) %collective-permute-start.1) | collective-permute-done | bytes 524320 | tf_op jit(solution)/shard_map/ppermute | solution.py:99
  169.1 0.2 fusion.49
  169.4 11.9 %collective-permute-done.2 = bf16[256,1024]{1,0:T(8,128)(2,1)} collective-permute-done((bf16[256,1024]{1,0:T(8,128)(2,1)}, bf16[256,1024]{1,0:T(8,128)(2,1)}, u32[]{:S(2)}, u32[]{:S(2)}) %collective-permute-start.2) | collective-permute-done | bytes 524320 | tf_op jit(solution)/shard_map/ppermute | solution.py:99
  181.3 1.1 constant_dynamic-update-slice_fusion.7
  182.4 1.1 constant_dynamic-update-slice_fusion.6
  183.7 1.2 constant_dynamic-update-slice_fusion.3
  185.0 1.2 constant_dynamic-update-slice_fusion.2
  186.5 0.7 fusion.38
  187.2 0.7 fusion.35
  187.9 0.7 slice-done.1
  188.7 2.3 %fusion.32 = bf16[256,1024]{1,0:T(8,128)(2,1)S(1)} fusion(bf16[4096,1024]{1,0:T(8,128)(2,1)S(1)} %bitcast.103, bf16[256,8192]{1,0:T(8,128)(2,1)S(1)} %constant_dynamic-update-slice_fusion, s32[]{:T(128)S(6)} %select_n.74), kind=kOutput, calls=%fused_computation.36 | convolution fusion | flops 2147745792 | bytes 11010052 | tf_op jit(solution)/shard_map/dot_general | solution.py:103
  191.0 1.2 reshape.194
  192.2 6.9 %all_gather.19 = bf16[1024,256]{1,0:T(8,128)(2,1)S(1)} all-gather(bf16[256,256]{1,0:T(8,128)(2,1)S(1)} %fusion.35), channel_id=1, replica_groups=mesh['doc'=2,'seq'=4,'head'=4] {'seq'}, dimensions={0}, use_global_device_ids=true | all-gather | bytes 655360 | tf_op jit(solution)/shard_map/all_gather | solution.py:114
  199.1 0.2 copy.44
  199.3 7.3 %all_gather.20 = bf16[1024,256]{1,0:T(8,128)(2,1)S(1)} all-gather(bf16[256,256]{1,0:T(8,128)(2,1)S(1)} %fusion.38), channel_id=1, replica_groups=mesh['doc'=2,'seq'=4,'head'=4] {'seq'}, dimensions={0}, use_global_device_ids=true | all-gather | bytes 655360 | tf_op jit(solution)/shard_map/all_gather | solution.py:113
  206.6 0.9 reshape.193
  207.5 2.7 %fusion.1 = (f32[256,2,4]{0,2,1:T(4,128)S(1)}, f32[2,1024,256,4]{2,1,3,0:T(8,128)S(1)}) fusion(pred[256,1024]{0,1:T(8,128)(4,1)S(1)} %fusion.49, bf16[256,2,4,128]{3,2,1,0:T(4,128)(2,1)} %reshape.194, bf16[1024,2,128,1]{2,1,0,3:T(2,128)(2,1)} %bitcast.100), kind=kOutput, calls=%fused_computation.5 | convolution fusion | flops 543160320 | bytes 9707520 | tf_op jit(solution)/shard_map/tkgd,rkd->tkgr/dot_general | solution.py:118
  210.2 2.0 fusion.2
  212.2 3.2 %fusion.11 = f32[2,128,256,4]{2,1,3,0:T(8,128)} fusion(bf16[1024,2,128,1]{0,2,3,1:T(8,128)(2,1)S(1)} %bitcast.99, f32[2,1024,256,4]{2,1,3,0:T(8,128)S(1)} %get-tuple-element.138, f32[256,2,4]{0,2,1:T(4,128)S(1)} %broadcast_maximum_fusion, pred[256,1024]{0,1:T(8,128)(4,1)S(1)} %fusion.49), kind=kOutput, calls=%fused_computation.15 | convolution fusion | flops 547356672 | bytes 10231808 | tf_op jit(solution)/shard_map/tkgr,rkd->tkgd/dot_general | solution.py:130
  215.5 1.6 copy.40
  217.2 0.3 div.27
  217.5 1.0 fusion.45
  (47 shorter events, 1.3 us)
Async XLA Ops:
  7.2 179.3 %copy-start = (bf16[4096,256]{1,0:T(8,128)(2,1)S(1)}, bf16[4096,256]{1,0:T(8,128)(2,1)}, u32[]{:S(2)}) copy-start(bf16[4096,256]{1,0:T(8,128)(2,1)} %param.26) | copy-start | bytes 6291460
  7.2 32.4 %all-gather.4.cloned.1.call-start = ((), (), s32[]{:S(2)}) async-start(), calls=%async_computation.2 | async-start | bytes 2621440 | tf_op jit(solution)/shard_map/all_gather | solution.py:14
  14.2 115.8 %reduce-scatter.2.cloned.1.call-start = ((), (), s32[]{:S(2)}) async-start(), calls=%async_computation.1 | async-start | bytes 5242880 | tf_op jit(solution)/shard_map/reduce_scatter | solution.py:87
  31.1 12.2 %copy-start.3 = (bf16[256,128]{1,0:T(8,128)(2,1)S(1)}, bf16[256,128]{1,0:T(8,128)(2,1)}, u32[]{:S(2)}) copy-start(bf16[256,128]{1,0:T(8,128)(2,1)} %param.19) | copy-start | bytes 196612
  53.0 77.0 %copy-start.2 = (bf16[256,1024]{1,0:T(8,128)(2,1)S(1)}, bf16[256,1024]{1,0:T(8,128)(2,1)}, u32[]{:S(2)}) copy-start(bf16[256,1024]{1,0:T(8,128)(2,1)} %param.16) | copy-start | bytes 1572868
  131.5 54.8 %copy-start.1 = (bf16[256,1024]{1,0:T(8,128)(2,1)}, bf16[256,1024]{1,0:T(8,128)(2,1)S(1)}, u32[]{:S(2)}) copy-start(bf16[256,1024]{1,0:T(8,128)(2,1)S(1)} %get-tuple-element.128) | copy-start | bytes 1572868
  142.7 13.6 %collective-permute-start = (bf16[256,1024]{1,0:T(8,128)(2,1)S(1)}, bf16[256,1024]{1,0:T(8,128)(2,1)S(1)}, u32[]{:S(2)}, u32[]{:S(2)}) collective-permute-start(bf16[256,1024]{1,0:T(8,128)(2,1)S(1)} %fusion.43), channel_id=1, source_target_pairs={{0,1},{1,2},{2,3},{3,0},{4,5},{5,6},{6,7},{7,4},{8,9},{9,10},{10,1... | collective-permute-start | bytes 1572872 | tf_op jit(solution)/shard_map/ppermute | solution.py:99
  156.3 12.8 %collective-permute-start.1 = (bf16[256,1024]{1,0:T(8,128)(2,1)S(1)}, bf16[256,1024]{1,0:T(8,128)(2,1)}, u32[]{:S(2)}, u32[]{:S(2)}) collective-permute-start(bf16[256,1024]{1,0:T(8,128)(2,1)S(1)} %collective-permute-done), channel_id=1, source_target_pairs={{0,1},{1,2},{2,3},{3,0},{4,5},{5,6},{6,7},{7,4},{8,9},{9,10},{10,1... | collective-permute-start | bytes 1572872 | tf_op jit(solution)/shard_map/ppermute | solution.py:99
  169.1 12.2 %collective-permute-start.2 = (bf16[256,1024]{1,0:T(8,128)(2,1)}, bf16[256,1024]{1,0:T(8,128)(2,1)}, u32[]{:S(2)}, u32[]{:S(2)}) collective-permute-start(bf16[256,1024]{1,0:T(8,128)(2,1)} %collective-permute-done.1), channel_id=1, source_target_pairs={{0,1},{1,2},{2,3},{3,0},{4,5},{5,6},{6,7},{7,4},{8,9},{9,10},{10,1... | collective-permute-start | bytes 1572872 | tf_op jit(solution)/shard_map/ppermute | solution.py:99
  183.5 4.5 %slice-start = ((s8[8388608]{0:T(1024)(128)(4,1)}), s8[4194304]{0:T(1024)(128)(4,1)S(1)}, s32[]{:S(2)}) async-start(s8[8388608]{0:T(1024)(128)(4,1)} %bitcast.102), calls=%async_computation.3 | async-start | bytes 8388608
  183.7 3.5 %copy-start.4 = (bf16[4096,256]{1,0:T(8,128)(2,1)S(1)}, bf16[4096,256]{1,0:T(8,128)(2,1)}, u32[]{:S(2)}) copy-start(bf16[4096,256]{1,0:T(8,128)(2,1)} %param.27) | copy-start | bytes 6291460
  186.5 2.2 slice-start.1
Sparse Core Ops, SparseCore 0:
  14.3 25.2 all-gather.3
  53.2 76.7 reduce-scatter.1
